TPU v7x, 8 devices: a whole 2x2x1 slice. The times are simulated.
8 devices in a mesh: data: 1 (over z), col: 2 (over y), row: 4 (over x, core).
Axes of the slice: x: 2, y: 2, z: 1, core: 2. Of those that a mesh axis runs over, the one named last changes fastest.
Arguments:
- residual: bfloat16 [256, 4096], P('data', 'row')
- gain_mlp: float32 [4096], P('row')
- gain_attn: float32 [4096], P('row')
- w_gate: bfloat16 [4096, 11008], P(None, ('col', 'row'))
- w_up: bfloat16 [4096, 11008], P(None, ('col', 'row'))
- w_down: bfloat16 [11008, 4096], P('col', 'row')
- w_qkv: bfloat16 [4096, 12288], P(None, ('col', 'row'))
Outputs:
- output 1: bfloat16 [256, 4096], P('data', 'row')
- output 2: bfloat16 [256, 12288], P('data', ('col', 'row'))
All inputs are finite; a program needn't handle non-finite values.
Results may differ from a plain program's by a relative error of at most 0.00403686.
Values are sent between devices in bfloat16 or wider.
A program may use at most 1 GiB of HBM per device.

v0:
```python
import jax
import jax.numpy as jnp
from jax import lax
from jax.sharding import PartitionSpec as P

NORM_EPS = 1e-6


def solution(mesh):
    row_size = mesh.shape['row']
    tok_spec = P('data', 'row')
    gain_spec = P('row')
    wide_spec = P(None, ('col', 'row'))
    down_spec = P('col', 'row')
    qkv_spec = P('data', ('col', 'row'))

    def shard_norm(shard, gain):
        shard_f = shard.astype(jnp.float32)
        sq_part = jnp.sum(shard_f * shard_f, axis=1, keepdims=True)
        sq_total = lax.psum(sq_part, 'row')
        row_scale = lax.rsqrt(sq_total / (shard.shape[1] * row_size) + NORM_EPS)
        return (shard_f * row_scale * gain).astype(jnp.bfloat16)

    def per_device(residual, gain_mlp, gain_attn, w_gate, w_up, w_down, w_qkv):
        normed = shard_norm(residual, gain_mlp)
        normed_full = lax.all_gather(normed, 'row', axis=1, tiled=True)
        gate_val = jnp.dot(normed_full, w_gate, preferred_element_type=jnp.float32)
        up_val = jnp.dot(normed_full, w_up, preferred_element_type=jnp.float32)
        act_val = (jax.nn.silu(gate_val) * up_val).astype(jnp.bfloat16)
        act_block = lax.all_gather(act_val, 'row', axis=1, tiled=True)
        down_part = jnp.dot(act_block, w_down, preferred_element_type=jnp.float32)
        down_sum = lax.psum(down_part, 'col')
        resid_next = (residual.astype(jnp.float32) + down_sum).astype(jnp.bfloat16)
        normed_next = shard_norm(resid_next, gain_attn)
        next_full = lax.all_gather(normed_next, 'row', axis=1, tiled=True)
        qkv_out = jnp.dot(next_full, w_qkv, preferred_element_type=jnp.float32).astype(jnp.bfloat16)
        return resid_next, qkv_out

    return jax.shard_map(per_device, mesh=mesh, in_specs=(tok_spec, gain_spec, gain_spec, wide_spec, wide_spec, down_spec, wide_spec), out_specs=(tok_spec, qkv_spec), check_vma=False)
```

profile of v0, /device:TPU:0, one launch (start us, length us, event | category | flops | bytes accessed | tf_op | source)
XLA Modules:
  0.0 167.0 jit_solution(10398497262187658326)
XLA Ops:
  7.2 0.0 all-gather.4.cloned.1.call-start
  7.2 1.2 fusion.4
  8.4 8.7 %psum.21 = f32[256,1]{0,1:T(1,128)S(1)} all-reduce(f32[256,1]{0,1:T(1,128)S(1)} %bitcast.15), channel_id=1, replica_groups=mesh['data'=1,'col'=2,'row'=4] {'row'}, use_global_device_ids=true, to_apply=%region_1.0 | all-reduce | flops 256 | bytes 2048 | tf_op jit(solution)/shard_map/psum | solution.py:20
  17.2 2.0 %fusion.6 = bf16[256,1024]{1,0:T(8,128)(2,1)} fusion(bf16[256,1024]{1,0:T(8,128)(2,1)} %param.7, f32[1024]{0:T(1024)} %param.8, f32[256]{0:T(256)S(1)} %bitcast.14), kind=kLoop, calls=%fused_computation.13 | loop fusion | flops 1048576 | bytes 1053696 | tf_op jit(solution)/shard_map/convert_element_type | solution.py:22
  19.2 0.0 all-gather.4.cloned.1.call-update
  19.2 0.0 all-gather.6.cloned.1.call-start
  19.3 19.7 %all-gather.4.cloned.1.call-done = bf16[256,4096]{1,0:T(8,128)(2,1)} async-done(((bf16[256,1024]{1,0:T(8,128)(2,1)}), bf16[256,4096]{1,0:T(8,128)(2,1)}) %all-gather.4.cloned.1.call-update) | async-done | bytes 2097168 | tf_op jit(solution)/shard_map/all_gather | solution.py:26
  39.0 0.0 copy-start.3
  39.0 8.0 %fusion.9 = f32[256,1376]{0,1:T(8,128)S(1)} fusion(bf16[256,4096]{1,0:T(8,128)(2,1)} %all-gather.4.cloned.1.call-done, bf16[4096,1376]{0,1:T(8,128)(2,1)} %param.10), kind=kOutput, calls=%fused_computation.17 | convolution fusion | flops 2885681152 | bytes 14778368 | tf_op jit(solution)/shard_map/dot_general | solution.py:27
  47.0 0.0 copy-done.3
  47.0 8.5 %fusion = bf16[256,1376]{0,1:T(8,128)(2,1)} fusion(bf16[256,4096]{1,0:T(8,128)(2,1)S(1)} %copy-done.3, bf16[4096,1376]{0,1:T(8,128)(2,1)} %param.11, f32[256,1376]{0,1:T(8,128)S(1)} %fusion.9), kind=kOutput, calls=%fused_computation.1 | convolution fusion | flops 2887794688 | bytes 15482880 | tf_op jit(solution)/shard_map/dot_general | solution.py:28
  55.5 0.0 all-gather.6.cloned.1.call-update
  55.5 0.0 copy-start
  55.5 0.0 all-reduce.2.cloned.1.call-start
  55.6 23.7 %all-gather.6.cloned.1.call-done = bf16[256,5504]{0,1:T(8,128)(2,1)} async-done(((bf16[256,1376]{0,1:T(8,128)(2,1)}), bf16[256,5504]{0,1:T(8,128)(2,1)}) %all-gather.6.cloned.1.call-update) | async-done | bytes 2818064 | tf_op jit(solution)/shard_map/all_gather | solution.py:30
  79.2 9.2 %fusion.10 = f32[256,1024]{1,0:T(8,128)} fusion(bf16[256,5504]{0,1:T(8,128)(2,1)} %all-gather.6.cloned.1.call-done, bf16[5504,1024]{1,0:T(8,128)(2,1)} %param.12), kind=kOutput, calls=%fused_computation.18 | convolution fusion | flops 2885681152 | bytes 15138816 | tf_op jit(solution)/shard_map/dot_general | solution.py:31
  88.4 0.0 copy-start.2
  88.4 0.0 all-reduce.2.cloned.1.call-update
  88.5 0.0 all-gather.8.cloned.1.call-start
  88.5 34.4 %all-reduce.2.cloned.1.call-done = f32[256,1024]{1,0:T(8,128)} async-done(((f32[256,1024]{1,0:T(8,128)}), f32[256,1024]{1,0:T(8,128)}) %all-reduce.2.cloned.1.call-update) | async-done | bytes 1048592 | tf_op jit(solution)/shard_map/psum | solution.py:32
  122.9 0.0 copy-done
  122.9 1.5 fusion.1
  124.3 0.0 copy-start.1
  124.4 6.3 %psum.23 = f32[256,1]{0,1:T(1,128)S(1)} all-reduce(f32[256,1]{0,1:T(1,128)S(1)} %bitcast.12), channel_id=1, replica_groups=mesh['data'=1,'col'=2,'row'=4] {'row'}, use_global_device_ids=true, to_apply=%region_4.5 | all-reduce | flops 256 | bytes 2048 | tf_op jit(solution)/shard_map/psum | solution.py:20
  130.7 0.0 copy-done.2
  130.7 1.0 fusion.3
  131.7 0.0 all-gather.8.cloned.1.call-update
  131.7 19.3 %all-gather.8.cloned.1.call-done = bf16[256,4096]{1,0:T(8,128)(2,1)} async-done(((bf16[256,1024]{1,0:T(8,128)(2,1)}), bf16[256,4096]{1,0:T(8,128)(2,1)}) %all-gather.8.cloned.1.call-update) | async-done | bytes 2097168 | tf_op jit(solution)/shard_map/all_gather | solution.py:35
  151.0 9.5 %convolution_convert_fusion = bf16[256,1536]{1,0:T(8,128)(2,1)} fusion(bf16[256,4096]{1,0:T(8,128)(2,1)} %all-gather.8.cloned.1.call-done, bf16[4096,1536]{1,0:T(8,128)(2,1)} %param.13), kind=kOutput, calls=%fused_computation.2 | convolution fusion | flops 3221618688 | bytes 15466496 | tf_op jit(solution)/shard_map/dot_general | solution.py:36
  160.5 0.0 copy-done.1
  (2 shorter events, 0.0 us)
Async XLA Ops:
  7.2 31.8 %all-gather.4.cloned.1.call-start = ((), (), s32[]{:S(2)}) async-start(), calls=%async_computation | async-start | bytes 2621440 | tf_op jit(solution)/shard_map/all_gather | solution.py:26
  19.2 60.0 %all-gather.6.cloned.1.call-start = ((), (), s32[]{:S(2)}) async-start(), calls=%async_computation.1 | async-start | bytes 3522560 | tf_op jit(solution)/shard_map/all_gather | solution.py:30
  39.0 8.0 %copy-start.3 = (bf16[256,4096]{1,0:T(8,128)(2,1)S(1)}, bf16[256,4096]{1,0:T(8,128)(2,1)}, u32[]{:S(2)}) copy-start(bf16[256,4096]{1,0:T(8,128)(2,1)} %all-gather.4.cloned.1.call-done) | copy-start | bytes 6291460
  55.5 67.4 %copy-start = (bf16[256,1024]{1,0:T(8,128)(2,1)S(1)}, bf16[256,1024]{1,0:T(8,128)(2,1)}, u32[]{:S(2)}) copy-start(bf16[256,1024]{1,0:T(8,128)(2,1)} %param.7) | copy-start | bytes 1572868
  55.5 67.3 %all-reduce.2.cloned.1.call-start = ((), (), s32[]{:S(2)}) async-start(), calls=%async_computation.2 | async-start | bytes 2097152 | tf_op jit(solution)/shard_map/psum | solution.py:32
  88.4 42.2 %copy-start.2 = (f32[1024]{0:T(1024)S(1)}, f32[1024]{0:T(1024)}, u32[]{:S(2)}) copy-start(f32[1024]{0:T(1024)} %param.9) | copy-start | bytes 12292
  88.5 62.5 %all-gather.8.cloned.1.call-start = ((), (), s32[]{:S(2)}) async-start(), calls=%async_computation.3 | async-start | bytes 2621440 | tf_op jit(solution)/shard_map/all_gather | solution.py:35
  124.3 36.2 %copy-start.1 = (bf16[256,1024]{1,0:T(8,128)(2,1)}, bf16[256,1024]{1,0:T(8,128)(2,1)S(1)}, u32[]{:S(2)}) copy-start(bf16[256,1024]{1,0:T(8,128)(2,1)S(1)} %get-tuple-element.3) | copy-start | bytes 1572868
Sparse Core Ops, SparseCore 0:
  19.4 19.5 all-gather.3
  55.6 23.5 all-gather.5
  88.6 34.2 all-reduce.1
  131.8 19.1 all-gather.7
where the time goes:
time: 167 us
  waiting for transfers between devices  97.1 us (58%)
  matrix products  35.2 us (21%)
  blocking collectives  15.1 us (9%)
  between operations  13.8 us (8%)
  other arithmetic  5.73 us (3%)
    psum x1, waiting for transfers between devices, per_device(): down_sum = lax.psum(down_part, 'col')  34.4 us
    all_gather x1, waiting for transfers between devices, per_device(): act_block = lax.all_gather(act_val, 'row', axis=1, tiled=True)  23.7 us
    all_gather x1, waiting for transfers between devices, per_device(): normed_full = lax.all_gather(normed, 'row', axis=1, tiled=True)  19.7 us
    all_gather x1, waiting for transfers between devices, per_device(): next_full = lax.all_gather(normed_next, 'row', axis=1, tiled=True)  19.3 us
    psum x2, blocking collectives, shard_norm(): sq_total = lax.psum(sq_part, 'row')  15.1 us
    dot_general x1, matrix products, per_device(): jnp.dot(next_full, w_qkv, preferred_element_type=jnp.float32)  9.5 us
    dot_general x1, matrix products, per_device(): down_part = jnp.dot(act_block, w_down, preferred_element_type=jnp.float32)  9.2 us
    dot_general x1, matrix products, per_device(): up_val = jnp.dot(normed_full, w_up, preferred_element_type=jnp.float32)  8.48 us
  transfers between devices with their start and end apart: 4, of which 4 were waited for; matrix products, arithmetic and copies ran while one was open for 0% of the time, Pallas kernels for 0%

commit v1 on v0

v1 whole, which is shorter than its diff:
```python
import functools

import jax
import jax.numpy as jnp
from jax import lax
from jax.experimental import pallas as pl
from jax.experimental.pallas import tpu as pltpu
from jax.sharding import PartitionSpec as P

NORM_EPS = 1e-6
MESH = pl.DeviceIdType.MESH
F32, BF16 = jnp.float32, jnp.bfloat16

X_PIECES = 4
GROUPS = ((0, 256), (256, 512), (768, 608))
CHUNKS = ((0, 64), (64, 64), (128, 64), (192, 64))
SENDS = (((0, 0), (0, 1), (0, 2), (0, 3)),
         ((1, 0), (1, 1)),
         ((2, 0), (2, 1), (1, 2), (2, 2), (1, 3), (2, 3)))
ORDER = tuple(b for s in SENDS for b in s)
W_PARTS = 8


def dot_t(a, b):
    return lax.dot_general(a, b, (((1,), (1,)), ((), ())), preferred_element_type=F32)


class Names:
    def __init__(self):
        self.table = {}

    def __call__(self, *key):
        return self.table.setdefault(key, len(self.table))


def kernel(tokens, width, ff, names, local_names,
           x_hbm, g1_hbm, g2_hbm, wg_hbm, wu_hbm, wd_hbm, wq_hbm, res_hbm, qkv_hbm,
           xg, nb, wg, wu, wd, wq, ag, acc, rbuf, xn, g1, g2, out, send_sem, recv_sem, loc_sem):
    data, y, row = lax.axis_index("data"), lax.axis_index("col"), lax.axis_index("row")
    cx = row // 2
    core = row - cx * 2
    sib_row = cx * 2 + 1 - core
    far_row = (1 - cx) * 2 + core
    fsib_row = (1 - cx) * 2 + 1 - core
    sib, far, fsib = (data, y, sib_row), (data, y, far_row), (data, y, fsib_row)
    up, diag = (data, 1 - y, row), (data, 1 - y, far_row)
    hidden = width * 4
    half = tokens // 2

    def remote(key, src, dst, dev):
        i = names(*key)
        return pltpu.make_async_remote_copy(src_ref=src, dst_ref=dst, send_sem=send_sem.at[i], recv_sem=recv_sem.at[i],
                                            device_id=dev, device_id_type=MESH)

    def local(key, src, dst):
        return pltpu.make_async_copy(src, dst, loc_sem.at[local_names(*key)])

    sent = []

    def go(copy):
        copy.start()
        sent.append(copy)
        return copy

    own = [local(("x",), x_hbm, xg.at[row]), local(("g1",), g1_hbm, g1.at[row]), local(("g2",), g2_hbm, g2.at[row])]
    for c in own:
        c.start()
    loads = {}
    for name, src, dst in (("wg", wg_hbm, wg), ("wu", wu_hbm, wu)):
        loads[name] = [local((name, i), src.at[pl.ds(c0, cn)], dst.at[pl.ds(c0, cn)]) for i, (c0, cn) in enumerate(GROUPS)]
    loads["wd"] = [local(("wd", i), wd_hbm.at[pl.ds(i * ff, ff)], wd.at[i]) for i in range(4)]
    part = hidden // W_PARTS
    loads["wq"] = [local(("wq", i), wq_hbm.at[pl.ds(i * part, part)], wq.at[pl.ds(i * part, part)]) for i in range(W_PARTS)]
    for pair in zip(loads["wg"], loads["wu"]):
        for c in pair:
            c.start()
    for name in ("wd", "wq"):
        for c in loads[name]:
            c.start()

    barrier = pltpu.get_barrier_semaphore()
    for dev in (sib, far, fsib, up, diag):
        pl.semaphore_signal(barrier, inc=1, device_id=dev, device_id_type=MESH)
    pl.semaphore_wait(barrier, 5)

    for c in own:
        c.wait()
    piece = half // X_PIECES

    def rows_of(side, p):
        return pl.ds(pl.multiple_of(side * half + p * piece, piece), piece)

    gains = []
    for tag, dev in (("s", sib), ("f", far), ("fs", fsib)):
        for name, ref in (("g1", g1), ("g2", g2)):
            gains.append(go(remote((name, tag), ref.at[row], ref.at[row], dev)))
    x_far = [go(remote(("xx", p), xg.at[row, rows_of(y, p)], xg.at[row, rows_of(y, p)], far)) for p in range(X_PIECES)]
    x_sib = go(remote(("xs",), xg.at[row], xg.at[row], sib))

    def norm(src, gain, rows0, count):
        def step(i, carry):
            rows = pl.ds(pl.multiple_of(rows0 + i * 16, 16), 16)
            blocks = [src[b, rows].astype(F32) for b in range(4)]
            total = sum(jnp.sum(v * v, axis=1, keepdims=True) for v in blocks)
            scale = lax.rsqrt(total / hidden + NORM_EPS)
            for b in range(4):
                nb[rows, b * width:(b + 1) * width] = (blocks[b] * scale * gain[b]).astype(BF16)
            return carry
        lax.fori_loop(0, count // 16, step, 0)

    x_up, x_fs = [], []

    def ready_direct(p):
        x_far[p].wait_recv()
        blk = xg.at[far_row, rows_of(y, p)]
        x_up.append(go(remote(("xy", p), blk, blk, up)))
        x_fs.append(go(remote(("xf", p), blk, blk, sib)))

    def ready_relayed(p):
        x_up[p].wait_recv()
        blk = xg.at[far_row, rows_of(1 - y, p)]
        x_fs.append(go(remote(("xf", X_PIECES + p), blk, blk, sib)))

    def norm_piece(q):
        x_fs[q].wait_recv()
        side, p = (y, q) if q < X_PIECES else (1 - y, q - X_PIECES)
        norm(xg, g1, side * half + p * piece, piece)

    for p in range(X_PIECES):
        ready_direct(p)
        if p == 0:
            for c in gains:
                c.wait_recv()
            x_sib.wait_recv()
        else:
            norm_piece(p - 1)
    for p in range(X_PIECES):
        ready_relayed(p)
        norm_piece(X_PIECES + p - 1)
    norm_piece(2 * X_PIECES - 1)

    a_sib, a_far, a_fs = {}, {}, {}
    for g, (c0, cn) in enumerate(GROUPS):
        cols = slice(c0, c0 + cn)
        loads["wg"][g].wait()
        loads["wu"][g].wait()
        gate = dot_t(wg[cols], nb[...])
        upv = dot_t(wu[cols], nb[...])
        ag[row, :, cols] = (jax.nn.silu(gate) * upv).astype(BF16).T
        for (gg, t) in SENDS[g]:
            t0, tn = CHUNKS[t]
            b0, bn = GROUPS[gg]
            blk = ag.at[row, pl.ds(t0, tn), pl.ds(b0, bn)]
            a_far[gg, t] = go(remote(("ax", gg, t), blk, blk, far))
        blk = ag.at[row, :, pl.ds(c0, cn)]
        a_sib[g] = go(remote(("as", g), blk, blk, sib))

    def forward(gg, t):
        a_far[gg, t].wait_recv()
        t0, tn = CHUNKS[t]
        b0, bn = GROUPS[gg]
        blk = ag.at[far_row, pl.ds(t0, tn), pl.ds(b0, bn)]
        a_fs[gg, t] = go(remote(("af", gg, t), blk, blk, sib))

    queue = list(ORDER)
    for _ in range(4):
        forward(*queue.pop(0))
    for c in loads["wd"]:
        c.wait()
    acc[...] = jnp.dot(ag[row], wd[row], preferred_element_type=F32)
    forward(*queue.pop(0))
    for c in a_sib.values():
        c.wait_recv()
    acc[...] += jnp.dot(ag[sib_row], wd[sib_row], preferred_element_type=F32)

    rs, xp, xf = {}, {}, {}

    def down(t):
        t0, tn = CHUNKS[t]
        need = max(queue.index(b) for b in queue if b[1] == t) if any(b[1] == t for b in queue) else -1
        for _ in range(need + 1):
            forward(*queue.pop(0))
        rows = slice(t0, t0 + tn)
        acc[rows] += jnp.dot(ag[far_row, rows], wd[far_row], preferred_element_type=F32)
        for g in range(len(GROUPS)):
            a_fs[g, t].wait_recv()
        acc[rows] += jnp.dot(ag[fsib_row, rows], wd[fsib_row], preferred_element_type=F32)
        hn = tn // 2
        src = acc.at[pl.ds(pl.multiple_of(t0 + (1 - y) * hn, hn), hn)]
        rs[t] = go(remote(("rs", t), src, rbuf.at[pl.ds(t0 // 2, hn)], up))

    def combine(t):
        t0, tn = CHUNKS[t]
        hn = tn // 2
        rs[t].wait_recv()
        rows = pl.ds(pl.multiple_of(t0 + y * hn, hn), hn)
        total = acc[rows] + rbuf[pl.ds(t0 // 2, hn)]
        xn[row, rows] = (xg[row, rows].astype(F32) + total).astype(BF16)
        blk = xn.at[row, rows]
        for tag, dev in (("x", far), ("d", diag), ("y", up), ("s", sib)):
            xp[tag, t] = go(remote(("xn", tag, t), blk, blk, dev))

    outs = []

    def collect(t):
        t0, tn = CHUNKS[t]
        hn = tn // 2
        mine = pl.ds(pl.multiple_of(t0 + y * hn, hn), hn)
        other = pl.ds(pl.multiple_of(t0 + (1 - y) * hn, hn), hn)
        for tag, r, rows in (("y", row, other), ("x", far_row, mine), ("d", far_row, other)):
            xp[tag, t].wait_recv()
            blk = xn.at[r, rows]
            xf[tag, t] = go(remote(("xf2", tag, t), blk, blk, sib))
        c = local(("res", t), xn.at[row, pl.ds(t0, tn)], res_hbm.at[pl.ds(t0, tn)])
        c.start()
        outs.append(c)

    def finish(t):
        t0, tn = CHUNKS[t]
        xp["s", t].wait_recv()
        for tag in ("y", "x", "d"):
            xf[tag, t].wait_recv()
        norm(xn, g2, t0, tn)

    def project(t0, tn, i):
        rows = slice(t0, t0 + tn)
        out[rows] = jnp.dot(nb[rows], wq[...], preferred_element_type=F32).astype(BF16)
        c = local(("qkv", i), out.at[pl.ds(t0, tn)], qkv_hbm.at[pl.ds(t0, tn)])
        c.start()
        outs.append(c)

    down(0)
    down(1)
    combine(0)
    down(2)
    combine(1)
    collect(0)
    down(3)
    combine(2)
    collect(1)
    for c in loads["wq"]:
        c.wait()
    finish(0)
    finish(1)
    project(0, 128, 0)
    combine(3)
    collect(2)
    finish(2)
    collect(3)
    finish(3)
    project(128, 128, 1)
    for c in sent:
        c.wait_send()
    for c in outs:
        c.wait()


def solution(mesh):
    def per_device(residual, gain_mlp, gain_attn, w_gate, w_up, w_down, w_qkv):
        tokens, width = residual.shape
        ff = w_gate.shape[1]
        qkv = w_qkv.shape[1]
        hidden = width * 4
        any_spec = pl.BlockSpec(memory_space=pl.ANY)
        return pl.pallas_call(
            functools.partial(kernel, tokens, width, ff, Names(), Names()),
            out_shape=(jax.ShapeDtypeStruct((tokens, width), BF16), jax.ShapeDtypeStruct((tokens, qkv), BF16)),
            in_specs=[any_spec] * 7,
            out_specs=(any_spec, any_spec),
            scratch_shapes=[
                pltpu.VMEM((4, tokens, width), BF16),
                pltpu.VMEM((tokens, hidden), BF16),
                pltpu.VMEM((ff, hidden), BF16),
                pltpu.VMEM((ff, hidden), BF16),
                pltpu.VMEM((4, ff, width), BF16),
                pltpu.VMEM((hidden, qkv), BF16),
                pltpu.VMEM((4, tokens, ff), BF16),
                pltpu.VMEM((tokens, width), F32),
                pltpu.VMEM((tokens // 2, width), F32),
                pltpu.VMEM((4, tokens, width), BF16),
                pltpu.VMEM((4, 1, width), F32),
                pltpu.VMEM((4, 1, width), F32),
                pltpu.VMEM((tokens, qkv), BF16),
                pltpu.SemaphoreType.DMA((96,)),
                pltpu.SemaphoreType.DMA((96,)),
                pltpu.SemaphoreType.DMA((48,)),
            ],
            compiler_params=pltpu.CompilerParams(collective_id=0, has_side_effects=True, vmem_limit_bytes=67_000_000),
            name="block",
        )(residual, gain_mlp.reshape(1, width), gain_attn.reshape(1, width), w_gate.T, w_up.T, w_down, w_qkv)

    return jax.shard_map(
        per_device, mesh=mesh,
        in_specs=(P('data', 'row'), P('row'), P('row'), P(None, ('col', 'row')), P(None, ('col', 'row')),
                  P('col', 'row'), P(None, ('col', 'row'))),
        out_specs=(P('data', 'row'), P('data', ('col', 'row'))), check_vma=False)
```

time: 167 us -> 64 us (0.38)
  waiting for transfers between devices: 97.1 us -> 0 us
  Pallas kernels: 0 us -> 58.9 us
  matrix products: 35.2 us -> 0 us
  blocking collectives: 15.1 us -> 0 us
  between operations: 13.8 us -> 0.64 us
  other arithmetic: 5.73 us -> 0 us
  local copies, waits for them, and re-layouts: 0.02 us -> 3.93 us
    all_gather x3 -> x0, waiting for transfers between devices: 62.7 us -> none  [the longest x1 23.7 us: per_device(): act_block = lax.all_gather(act_val, 'row', axis=1, tiled=True)]
    pallas_call x0 -> x1, Pallas kernels: none -> 58.9 us  [per_device(): pl.pallas_call(functools.partial(kernel, tokens, width, ff, Names(), Name...]
    dot_general x4 -> x0, matrix products: 35.2 us -> none  [the longest x1 9.5 us: per_device(): jnp.dot(next_full, w_qkv, preferred_element_type=jnp.float32)]
    psum x1 -> x0, waiting for transfers between devices: 34.4 us -> none  [per_device(): down_sum = lax.psum(down_part, 'col')]
    psum x2 -> x0, blocking collectives: 15.1 us -> none  [shard_norm(): sq_total = lax.psum(sq_part, 'row')]
    unnamed x8 -> x2, local copies, waits for them, and re-layouts: 0.02 us -> 3.93 us
    convert_element_type x2 -> x0, other arithmetic: 3.02 us -> none  [shard_norm(): return (shard_f * row_scale * gain).astype(jnp.bfloat16)]
    reduce_sum x2 -> x0, other arithmetic: 2.69 us -> none  [shard_norm(): sq_part = jnp.sum(shard_f * shard_f, axis=1, keepdims=True)]
  transfers between devices with their start and end apart: 4 -> 0, of which waited for: 4 -> 0; matrix products, arithmetic and copies ran while one was open for 0% -> 0% of each run, Pallas kernels for 0% -> 0%
where the time goes in v1:
time: 64 us; the launch traced here: 63.5 us
  Pallas kernels  58.9 us (92%)
  local copies, waits for them, and re-layouts  3.93 us (6%)
  between operations  0.64 us (1%)
    pallas_call x1, Pallas kernels, per_device(): pl.pallas_call(functools.partial(kernel, tokens, width, ff, Names(), Name...  58.9 us
    unnamed x2, local copies, waits for them, and re-layouts  3.93 us

profile of v1, /device:TPU:0, one launch (start us, length us, event | category | flops | bytes accessed | tf_op | source)
XLA Modules:
  0.0 63.5 jit_solution(10513376436063488916)
XLA Ops:
  0.6 58.9 %block.1 = (bf16[256,1024]{1,0:T(8,128)(2,1)}, bf16[256,1536]{1,0:T(8,128)(2,1)}) custom-call(bf16[256,1024]{1,0:T(8,128)(2,1)} %x_hbm.1, f32[1,1024]{1,0:T(1,128)} %bitcast.6, f32[1,1024]{1,0:T(1,128)} %bitcast.7, bf16[1376,4096]{1,0:T(8,128)(2,1)} %bitcast.4, bf16[1376,4096]{1,0:T(8,128)(2,1)} %bitcast.5, bf16[5504,1024]{1,0:T(8,128)(2,1)} %wd_hbm.1, ...), custom_call_target="tpu_custom_call" | custom-call | tf_op jit(solution)/shard_map/block/pallas_call | solution.py:265
  59.5 1.9 %copy.11 = bf16[256,1024]{1,0:T(8,128)(2,1)} copy(bf16[256,1024]{1,0:T(8,128)(2,1)} %get-tuple-element.4) | data formatting | bytes 1048576
  61.4 2.1 %copy.12 = bf16[256,1536]{1,0:T(8,128)(2,1)} copy(bf16[256,1536]{1,0:T(8,128)(2,1)} %get-tuple-element.5) | data formatting | bytes 1572864

commit v2 on v0

v2 whole, which is shorter than its diff:
```python
import functools

import jax
import jax.numpy as jnp
from jax import lax
from jax.experimental import pallas as pl
from jax.experimental.pallas import tpu as pltpu
from jax.sharding import PartitionSpec as P

NORM_EPS = 1e-6
MESH = pl.DeviceIdType.MESH
F32, BF16 = jnp.float32, jnp.bfloat16

SLICE = 128
RELAYED, DIRECT = 3, 5
NEAR = ((0, 352), (352, 336), (688, 352), (1040, 336))
WIDE = ((0, 688), (688, 688))
GROUPS = ((0, 384), (384, 384), (768, 384), (1152, 224))
BESIDE = ((("d", 0, 0),), (("d", 0, 1),), (("d", 1, 0),), (("d", 1, 1),), (("d", 2, 0), ("d", 2, 1), ("r", 0, 0), ("r", 0, 1)))
PASSES = (((("d", 0), ("d", 1)), ((), (("r", 1, 0),))),
          ((("d", 2), ("r", 0)), ((("d", 3, None),), (("r", 1, 1), ("r", 2, 0), ("d", 4, None)))),
          ((("d", 3), ("r", 1)), ((("r", 2, 1),), ())),
          ((("d", 4), ("r", 2)), ()))
CHUNK, CHUNKS = 32, 8
SPLIT_CHUNKS = (0,)
DIRECT_DIAG = (7,)
CUT = 4
STEPS = (
    "fwd0", "dfar0", "dfs0", "fwd1", "dfar1", "dfs1", "fwd2", "dfar2", "dfs2", "comb0", "fwd3", "dfar3",
    "dfs3", "comb1", "fwd4", "dfar4", "dfs4", "comb2", "fwd5", "dfar5", "cy0", "dfs5", "comb3", "fwd6",
    "dfar6", "cy1", "dfs6", "fwd7", "dfar7", "comb4", "cx0", "cy2", "dfs7", "cx1", "cx2", "comb5",
    "cd0", "cy3", "cx3", "fin0", "cd1", "comb6", "cx4", "cy4", "fin1", "cd2", "cx5", "comb7",
    "fin2", "cd3", "cy5", "cx6", "cy6", "fin3", "proj0", "cy7", "cd4", "cx7", "cd5", "cd7",
    "fin4", "cd6", "fin5", "fin7", "fin6", "proj1",
)
W_PARTS = 8


def dot(a, b):
    return jnp.dot(a, b, preferred_element_type=F32)


def dot_t(a, b):
    return lax.dot_general(a, b, (((1,), (1,)), ((), ())), preferred_element_type=F32)


def scoped(fn):
    @functools.wraps(fn)
    def run(*args):
        with jax.named_scope("#".join([fn.__name__] + [str(a) for a in args])):
            return fn(*args)
    return run


class Names:
    def __init__(self):
        self.table = {}

    def __call__(self, *key):
        return self.table.setdefault(key, len(self.table))


def kernel(tokens, width, ff, names, local_names,
           x_hbm, g1_hbm, g2_hbm, wg_hbm, wu_hbm, wd_hbm, wq_hbm, res, out,
           xg, nb, wg, wu, wd, wq, ag, acc, rbuf, xn, g1, g2, sq, scale, gacc, uacc, send_sem, recv_sem, loc_sem):
    data, y, row = lax.axis_index("data"), lax.axis_index("col"), lax.axis_index("row")
    cx = row // 2
    core = row - cx * 2
    sib_row = cx * 2 + 1 - core
    far_row = (1 - cx) * 2 + core
    fsib_row = (1 - cx) * 2 + 1 - core
    sib, far, fsib = (data, y, sib_row), (data, y, far_row), (data, y, fsib_row)
    up, diag = (data, 1 - y, row), (data, 1 - y, far_row)
    hidden = width * 4
    slices = width // SLICE

    def remote(key, src, dst, dev):
        i = names(*key)
        return pltpu.make_async_remote_copy(src_ref=src, dst_ref=dst, send_sem=send_sem.at[i], recv_sem=recv_sem.at[i],
                                            device_id=dev, device_id_type=MESH)

    def local(key, src, dst):
        return pltpu.make_async_copy(src, dst, loc_sem.at[local_names(*key)])

    sent = []

    def go(key, ref, dev):
        copy = remote(key, ref, ref, dev)
        copy.start()
        sent.append(copy)
        return copy

    own = [local(("x",), x_hbm, xg.at[row]), local(("g1",), g1_hbm, g1.at[row]), local(("g2",), g2_hbm, g2.at[row])]
    for c in own:
        c.start()
    loads = {}
    for name, src, dst in (("wg", wg_hbm, wg), ("wu", wu_hbm, wu)):
        loads[name] = [local((name, i), src.at[pl.ds(c0, cn)], dst.at[pl.ds(c0, cn)]) for i, (c0, cn) in enumerate(NEAR)]
    loads["wd"] = [local(("wd", i), wd_hbm.at[pl.ds(i * ff, ff)], wd.at[i]) for i in range(4)]
    part = hidden // W_PARTS
    loads["wq"] = [local(("wq", i), wq_hbm.at[pl.ds(i * part, part)], wq.at[pl.ds(i * part, part)]) for i in range(W_PARTS)]
    for pair in zip(loads["wg"], loads["wu"]):
        for c in pair:
            c.start()
    for name in ("wd", "wq"):
        for c in loads[name]:
            c.start()

    barrier = pltpu.get_barrier_semaphore()
    for dev in (sib, far, fsib, up, diag):
        pl.semaphore_signal(barrier, inc=1, device_id=dev, device_id_type=MESH)

    with jax.named_scope("own"):
        for c in own:
            c.wait()
        total = jnp.concatenate(
            [jnp.sum(jnp.square(xg[row, i:i + 64].astype(F32)), axis=1, keepdims=True) for i in range(0, tokens, 64)], axis=0)
        sq[row] = jnp.broadcast_to(total, (tokens, 128)).T[0:8]
    with jax.named_scope("barrier"):
        pl.semaphore_wait(barrier, 5)

    def cut(k):
        return pl.ds(pl.multiple_of(k * SLICE, SLICE), SLICE)

    def direct_slice(p):
        return y * (slices - RELAYED) + p if p < RELAYED else p

    def relayed_slice(q):
        return (1 - y) * (slices - RELAYED) + q

    def slice_of(item):
        return direct_slice(item[1]) if item[0] == "d" else relayed_slice(item[1])

    def parts(item):
        return (0, 1) if item[0] == "r" or item[1] < RELAYED else (None,)

    def x_block(b, item):
        toks = slice(None) if item[2] is None else pl.ds(item[2] * (tokens // 2), tokens // 2)
        return xg.at[b, toks, cut(slice_of(item))]

    gains = {}
    for name, ref in (("g1", g1), ("g2", g2)):
        for tag, dev in (("s", sib), ("f", far), ("fs", fsib)):
            gains[name, tag] = remote((name, tag), ref.at[row], ref.at[row], dev)
    small = [go(("sq", tag), sq.at[row], dev) for tag, dev in (("f", far), ("fs", fsib), ("s", sib))]
    x_sib = go(("xs",), xg.at[row], sib)
    x_in, x_fs = {}, {}
    for p in range(DIRECT):
        for h in parts(("d", p)):
            x_in["d", p, h] = go(("xx", p, h), x_block(row, ("d", p, h)), far)
        if p == 0:
            for c in gains.values():
                c.start()
                sent.append(c)

    def norm_slice(b, k):
        cols = pl.ds(pl.multiple_of(b * width + k * SLICE, SLICE), SLICE)
        nb[:, cols] = (xg[b, :, cut(k)].astype(F32) * scale[...] * g1[b, :, cut(k)]).astype(BF16)

    def norm_block(b):
        def step(k, carry):
            norm_slice(b, k)
            return carry
        lax.fori_loop(0, slices, step, 0)

    @scoped
    def relay(*item):
        x_in[item].wait_recv()
        blk = x_block(far_row, item)
        kind, p, h = item
        if kind == "d" and p < RELAYED:
            x_in["r", p, h] = go(("xy", p, h), blk, up)
        x_fs[item] = go(("xf",) + item, blk, sib)

    with jax.named_scope("stats"):
        for c in small:
            c.wait_recv()
        mean = (sq[0] + sq[1] + sq[2] + sq[3]) / hidden
        scale[...] = jnp.broadcast_to(lax.rsqrt(mean + NORM_EPS)[0:1], (128, tokens)).T
    with jax.named_scope("norm_own"):
        norm_block(row)
    with jax.named_scope("norm_sib"):
        gains["g1", "s"].wait_recv()
        x_sib.wait_recv()
        norm_block(sib_row)

    near = pl.ds(pl.multiple_of(cx * 2 * width, 2 * width), 2 * width)
    for item in BESIDE[0]:
        relay(*item)
    for g, (c0, cn) in enumerate(NEAR):
        cols = slice(c0, c0 + cn)
        with jax.named_scope(f"gu_near#{g}"):
            loads["wg"][g].wait()
            loads["wu"][g].wait()
            gacc[cols] = dot_t(wg[cols, near], nb[:, near])
            uacc[cols] = dot_t(wu[cols, near], nb[:, near])
        for item in BESIDE[1 + g]:
            relay(*item)
    for tag in ("f", "fs"):
        gains["g1", tag].wait_recv()

    a_sib, a_far, a_fs = {}, {}, {}

    def a_blocks(t):
        return [(g, c0, cn) for g, (c0, cn) in enumerate(GROUPS)] if t in SPLIT_CHUNKS else [(None, 0, ff)]

    def send_a(t, g, c0, cn):
        t0, tn = t * CHUNK, CHUNK
        a_far[t, g] = go(("ax", t, g), ag.at[row, pl.ds(t0, tn), pl.ds(c0, cn)], far)

    for i, (items, relays) in enumerate(PASSES):
        with jax.named_scope(f"norm_pass#{i}"):
            for item in items:
                norm_slice(far_row, slice_of(item))
            for item in items:
                for h in parts(item):
                    x_fs[item + (h,)].wait_recv()
                norm_slice(fsib_row, slice_of(item))
        where = [pl.ds(pl.multiple_of(b * width + slice_of(item) * SLICE, SLICE), SLICE)
                 for item in items for b in (far_row, fsib_row)]

        def product(w, cols):
            return dot_t(jnp.concatenate([w[cols, k] for k in where], axis=1), jnp.concatenate([nb[:, k] for k in where], axis=1))

        if i < len(PASSES) - 1:
            for g, (c0, cn) in enumerate(WIDE):
                cols = slice(c0, c0 + cn)
                with jax.named_scope(f"gu_pass#{i}#{g}"):
                    gate, upv = product(wg, cols), product(wu, cols)
                    gacc[cols] += gate
                    uacc[cols] += upv
                for item in relays[g]:
                    relay(*item)
            continue
        for g, (c0, cn) in enumerate(GROUPS):
            with jax.named_scope(f"gu_last#{g}"):
                cols = slice(c0, c0 + cn)
                gate = gacc[cols] + product(wg, cols)
                upv = uacc[cols] + product(wu, cols)
                ag[row, :, cols] = (jax.nn.silu(gate) * upv).astype(BF16).T
            for t in SPLIT_CHUNKS:
                send_a(t, g, c0, cn)
            a_sib[g] = go(("as", g), ag.at[row, :, pl.ds(c0, cn)], sib)
    for t in range(CHUNKS):
        if t not in SPLIT_CHUNKS:
            send_a(t, None, 0, ff)

    @scoped
    def forward(t):
        t0, tn = t * CHUNK, CHUNK
        for g, c0, cn in a_blocks(t):
            a_far[t, g].wait_recv()
            a_fs[t, g] = go(("af", t, g), ag.at[far_row, pl.ds(t0, tn), pl.ds(c0, cn)], sib)

    for c in loads["wd"]:
        c.wait()
    with jax.named_scope("down_own"):
        acc[...] = dot(ag[row], wd[row])
    with jax.named_scope("down_sib"):
        for c in a_sib.values():
            c.wait_recv()
        acc[...] += dot(ag[sib_row], wd[sib_row])

    rs, xp, xf = {}, {}, {}

    def halves(t):
        t0, tn = t * CHUNK, CHUNK
        hn = tn // 2
        return (pl.ds(pl.multiple_of(t0 + y * hn, hn), hn), pl.ds(pl.multiple_of(t0 + (1 - y) * hn, hn), hn),
                pl.ds(t0 // 2, hn))

    @scoped
    def down_far(t):
        rows = slice(t * CHUNK, (t + 1) * CHUNK)
        acc[rows] += dot(ag[far_row, rows], wd[far_row])

    @scoped
    def down_fsib(t):
        rows = slice(t * CHUNK, (t + 1) * CHUNK)
        for g, _, _ in a_blocks(t):
            a_fs[t, g].wait_recv()
        acc[rows] += dot(ag[fsib_row, rows], wd[fsib_row])
        _, other, packed = halves(t)
        rs[t] = remote(("rs", t), acc.at[other], rbuf.at[packed], up)
        rs[t].start()
        sent.append(rs[t])

    @scoped
    def combine(t):
        mine, _, packed = halves(t)
        rs[t].wait_recv()
        xn[row, mine] = (xg[row, mine].astype(F32) + (acc[mine] + rbuf[packed])).astype(BF16)
        blk = xn.at[row, mine]
        targets = [("y", up), ("x", far), ("s", sib)] + ([("d", diag)] if t in DIRECT_DIAG else [])
        for tag, dev in targets:
            xp[tag, t] = go(("xn", tag, t), blk, dev)

    @scoped
    def collect(tag, t):
        mine, other, _ = halves(t)
        r, rows = {"y": (row, other), "x": (far_row, mine), "d": (far_row, other)}[tag]
        xp[tag, t].wait_recv()
        blk = xn.at[r, rows]
        if tag == "y" and t not in DIRECT_DIAG:
            xp["d", t] = go(("xn", "d", t), blk, far)
        xf[tag, t] = go(("xf2", tag, t), blk, sib)

    @scoped
    def finish(t):
        t0, tn = t * CHUNK, CHUNK
        xp["s", t].wait_recv()
        for tag in ("y", "x", "d"):
            xf[tag, t].wait_recv()
        res[pl.ds(t0, tn)] = xn[row, pl.ds(t0, tn)]

        def step(i, carry):
            rows = pl.ds(pl.multiple_of(t0 + i * 16, 16), 16)
            blocks = [xn[b, rows].astype(F32) for b in range(4)]
            total = sum(jnp.sum(v * v, axis=1, keepdims=True) for v in blocks)
            r = lax.rsqrt(total / hidden + NORM_EPS)
            for b in range(4):
                nb[rows, b * width:(b + 1) * width] = (blocks[b] * r * g2[b]).astype(BF16)
            return carry
        lax.fori_loop(0, tn // 16, step, 0)

    @scoped
    def project(i):
        if i == 0:
            for c in loads["wq"]:
                c.wait()
        rows = slice(0, CUT * CHUNK) if i == 0 else slice(CUT * CHUNK, tokens)
        out[rows] = dot(nb[rows], wq[...]).astype(BF16)

    for tag in ("s", "f", "fs"):
        gains["g2", tag].wait_recv()
    steps = {"fwd": forward, "dfar": down_far, "dfs": down_fsib, "comb": combine, "cy": functools.partial(collect, "y"),
             "cx": functools.partial(collect, "x"), "cd": functools.partial(collect, "d"), "fin": finish, "proj": project}
    for name in STEPS:
        steps[name[:-1]](int(name[-1]))
    with jax.named_scope("drain"):
        for c in sent:
            c.wait_send()


def solution(mesh):
    def per_device(residual, gain_mlp, gain_attn, w_gate, w_up, w_down, w_qkv):
        tokens, width = residual.shape
        ff = w_gate.shape[1]
        qkv = w_qkv.shape[1]
        hidden = width * 4
        any_spec = pl.BlockSpec(memory_space=pl.ANY)
        return pl.pallas_call(
            functools.partial(kernel, tokens, width, ff, Names(), Names()),
            out_shape=(pltpu.VMEM((tokens, width), BF16), pltpu.VMEM((tokens, qkv), BF16)),
            in_specs=[any_spec] * 7,
            out_specs=(pl.BlockSpec(memory_space=pltpu.VMEM),) * 2,
            scratch_shapes=[
                pltpu.VMEM((4, tokens, width), BF16),
                pltpu.VMEM((tokens, hidden), BF16),
                pltpu.VMEM((ff, hidden), BF16),
                pltpu.VMEM((ff, hidden), BF16),
                pltpu.VMEM((4, ff, width), BF16),
                pltpu.VMEM((hidden, qkv), BF16),
                pltpu.VMEM((4, tokens, ff), BF16),
                pltpu.VMEM((tokens, width), F32),
                pltpu.VMEM((tokens // 2, width), F32),
                pltpu.VMEM((4, tokens, width), BF16),
                pltpu.VMEM((4, 1, width), F32),
                pltpu.VMEM((4, 1, width), F32),
                pltpu.VMEM((4, 8, tokens), F32),
                pltpu.VMEM((tokens, 128), F32),
                pltpu.VMEM((ff, tokens), F32),
                pltpu.VMEM((ff, tokens), F32),
                pltpu.SemaphoreType.DMA((160,)),
                pltpu.SemaphoreType.DMA((160,)),
                pltpu.SemaphoreType.DMA((32,)),
            ],
            compiler_params=pltpu.CompilerParams(collective_id=0, has_side_effects=True, vmem_limit_bytes=65_500_000),
            name="block",
        )(residual, gain_mlp.reshape(1, width), gain_attn.reshape(1, width), w_gate.T, w_up.T, w_down, w_qkv)

    return jax.shard_map(
        per_device, mesh=mesh,
        in_specs=(P('data', 'row'), P('row'), P('row'), P(None, ('col', 'row')), P(None, ('col', 'row')),
                  P('col', 'row'), P(None, ('col', 'row'))),
        out_specs=(P('data', 'row'), P('data', ('col', 'row'))), check_vma=False)
```

time: 167 us -> 55.3 us (0.33)
  waiting for transfers between devices: 97.1 us -> 0 us
  Pallas kernels: 0 us -> 52.9 us
  matrix products: 35.2 us -> 0 us
  blocking collectives: 15.1 us -> 0 us
  between operations: 13.8 us -> 0.64 us
  other arithmetic: 5.73 us -> 0 us
    all_gather x3 -> x0, waiting for transfers between devices: 62.7 us -> none  [the longest x1 23.7 us: per_device(): act_block = lax.all_gather(act_val, 'row', axis=1, tiled=True)]
    pallas_call x0 -> x1, Pallas kernels: none -> 52.9 us  [per_device(): pl.pallas_call(functools.partial(kernel, tokens, width, ff, Names(), Name...]
    dot_general x4 -> x0, matrix products: 35.2 us -> none  [the longest x1 9.5 us: per_device(): jnp.dot(next_full, w_qkv, preferred_element_type=jnp.float32)]
    psum x1 -> x0, waiting for transfers between devices: 34.4 us -> none  [per_device(): down_sum = lax.psum(down_part, 'col')]
    psum x2 -> x0, blocking collectives: 15.1 us -> none  [shard_norm(): sq_total = lax.psum(sq_part, 'row')]
    convert_element_type x2 -> x0, other arithmetic: 3.02 us -> none  [shard_norm(): return (shard_f * row_scale * gain).astype(jnp.bfloat16)]
    reduce_sum x2 -> x0, other arithmetic: 2.69 us -> none  [shard_norm(): sq_part = jnp.sum(shard_f * shard_f, axis=1, keepdims=True)]
  transfers between devices with their start and end apart: 4 -> 0, of which waited for: 4 -> 0; matrix products, arithmetic and copies ran while one was open for 0% -> 0% of each run, Pallas kernels for 0% -> 0%
where the time goes in v2:
time: 55.3 us; the launch traced here: 55.2 us
  Pallas kernels  52.9 us (96%)
  local copies, waits for them, and re-layouts  1.67 us (3%)
  between operations  0.64 us (1%)
    pallas_call x1, Pallas kernels, per_device(): pl.pallas_call(functools.partial(kernel, tokens, width, ff, Names(), Name...  52.9 us
    unnamed x2, local copies, waits for them, and re-layouts  1.67 us

profile of v2, /device:TPU:0, one launch (start us, length us, event | category | flops | bytes accessed | tf_op | source)
XLA Modules:
  0.0 55.2 jit_solution(17545455478981236123)
XLA Ops:
  0.6 52.9 %block.1 = (bf16[256,1024]{1,0:T(8,128)(2,1)S(1)}, bf16[256,1536]{1,0:T(8,128)(2,1)S(1)}) custom-call(bf16[256,1024]{1,0:T(8,128)(2,1)} %x_hbm.1, f32[1,1024]{1,0:T(1,128)} %bitcast.6, f32[1,1024]{1,0:T(1,128)} %bitcast.7, bf16[1376,4096]{1,0:T(8,128)(2,1)} %bitcast.4, bf16[1376,4096]{1,0:T(8,128)(2,1)} %bitcast.5, bf16[5504,1024]{1,0:T(8,128)(2,1)} %wd_hbm.1, ...), custom_call_target="tpu_custom_call" | custom-call | tf_op jit(solution)/shard_map/block/pallas_call | solution.py:352
  53.6 0.8 %copy.11 = bf16[256,1024]{1,0:T(8,128)(2,1)} copy(bf16[256,1024]{1,0:T(8,128)(2,1)S(1)} %get-tuple-element.2) | data formatting | bytes 1048576
  54.4 0.9 %copy.12 = bf16[256,1536]{1,0:T(8,128)(2,1)} copy(bf16[256,1536]{1,0:T(8,128)(2,1)S(1)} %get-tuple-element.3) | data formatting | bytes 1572864

commit v3 on v2

v3 whole, which is shorter than its diff:
```python
import functools
import math

import jax
import jax.numpy as jnp
from jax import lax
from jax.experimental import pallas as pl
from jax.experimental.pallas import tpu as pltpu
from jax.sharding import PartitionSpec as P

NORM_EPS = 1e-6
MESH = pl.DeviceIdType.MESH
F32, BF16 = jnp.float32, jnp.bfloat16

SLICE = 128
RELAYED, DIRECT = 3, 5
NEAR = ((0, 352), (352, 336), (688, 352), (1040, 336))
WIDE = ((0, 688), (688, 688))
GROUPS = ((0, 384), (384, 384), (768, 384), (1152, 224))
BESIDE = ((("d", 0, 0),), (("d", 0, 1),), (("d", 1, 0),), (("d", 1, 1), ("d", 2, 0)), (("d", 2, 1), ("r", 0, 0)))
PASSES = (((("d", 0), ("d", 1)), ((("r", 0, 1),), (("r", 1, 0), ("d", 3, None)))),
          ((("d", 2), ("r", 0)), ((("r", 1, 1),), (("d", 4, None), ("r", 2, 0)))),
          ((("d", 3), ("r", 1)), ((("r", 2, 1),), ())),
          ((("d", 4), ("r", 2)), ()))
CHUNK, CHUNKS = 32, 8
SPLIT_CHUNKS = (0,)
DIAGONAL = "xxxxxydd"
CUT = 4
STEPS = (
    "fwd0", "dfar0", "dfs0", "fwd1", "dfar1", "dfs1", "fwd2", "dfar2", "dfs2", "comb0", "fwd3", "dfar3",
    "dfs3", "comb1", "fwd4", "dfar4", "dfs4", "comb2", "fwd5", "dfar5", "cy0", "dfs5", "comb3", "fwd6",
    "dfar6", "cy1", "dfs6", "fwd7", "dfar7", "comb4", "cx0", "cy2", "dfs7", "cx1", "cx2", "comb5",
    "cd0", "cy3", "cx3", "fin0", "cd1", "comb6", "cx4", "cy4", "fin1", "cd2", "cx5", "comb7",
    "fin2", "cd3", "cy5", "cx6", "cy6", "fin3", "proj0", "cy7", "cd4", "cd5", "cd6", "cx7",
    "fin4", "cd7", "fin5", "fin6", "fin7",
)
W_PARTS = 8


def dot(a, b):
    return jnp.dot(a, b, preferred_element_type=F32)


def dot_t(a, b):
    return lax.dot_general(a, b, (((1,), (1,)), ((), ())), preferred_element_type=F32)


def scoped(fn):
    @functools.wraps(fn)
    def run(*args):
        with jax.named_scope("#".join([fn.__name__] + [str(a) for a in args])):
            return fn(*args)
    return run


class Names:
    def __init__(self):
        self.table = {}

    def __call__(self, *key):
        return self.table.setdefault(key, len(self.table))


def kernel(tokens, width, ff, names, local_names,
           x_hbm, g1_hbm, g2_hbm, wg_hbm, wu_hbm, wd_hbm, wq_hbm, res, out, nb, wq,
           xg, wg, wu, wd, ag, acc, rbuf, xn, gains, sq, scale, gacc, uacc, send_sem, recv_sem, loc_sem):
    data, y, row = lax.axis_index("data"), lax.axis_index("col"), lax.axis_index("row")
    cx = row // 2
    core = row - cx * 2
    sib_row = cx * 2 + 1 - core
    far_row = (1 - cx) * 2 + core
    fsib_row = (1 - cx) * 2 + 1 - core
    sib, far, fsib = (data, y, sib_row), (data, y, far_row), (data, y, fsib_row)
    up, diag = (data, 1 - y, row), (data, 1 - y, far_row)
    hidden = width * 4
    wide = ag.shape[2]
    slices = width // SLICE

    def remote(key, src, dst, dev):
        return pltpu.make_async_remote_copy(src_ref=src, dst_ref=dst, send_sem=send_sem.at[1 if key[0] == "sq" else 0], recv_sem=recv_sem.at[names(*key)],
                                            device_id=dev, device_id_type=MESH)

    def local(key, src, dst):
        return pltpu.make_async_copy(src, dst, loc_sem.at[local_names(*key)])

    def arrived(key, like):
        pltpu.make_async_copy(like, like, recv_sem.at[names(*key)]).wait()

    def loaded(key, like):
        pltpu.make_async_copy(like, like, loc_sem.at[local_names(*key)]).wait()

    sent = []

    def go(key, ref, dev, dst=None):
        copy = remote(key, ref, ref if dst is None else dst, dev)
        copy.start()
        if key[0] != "sq":
            sent.append(math.prod(ref.shape) * jnp.dtype(ref.dtype).itemsize)
        return copy

    own = [local(("x",), x_hbm, xg.at[row]), local(("g1",), g1_hbm, gains.at[row, 0]), local(("g2",), g2_hbm, gains.at[row, 1])]
    for c in own:
        c.start()
    for g, (c0, cn) in enumerate(NEAR):
        for src, dst in ((wg_hbm, wg), (wu_hbm, wu)):
            local(("w", g), src.at[pl.ds(c0, cn)], dst.at[pl.ds(c0, cn)]).start()
    for i in range(4):
        local(("wd",), wd_hbm.at[pl.ds(i * ff, ff)], wd.at[i]).start()
    part = hidden // W_PARTS
    for i in range(W_PARTS):
        local(("wq",), wq_hbm.at[pl.ds(i * part, part)], wq.at[pl.ds(i * part, part)]).start()

    barrier = pltpu.get_barrier_semaphore()
    for dev in (sib, far, fsib, up, diag):
        pl.semaphore_signal(barrier, inc=1, device_id=dev, device_id_type=MESH)

    with jax.named_scope("own"):
        if wide > ff:
            ag[row, :, ff:] = jnp.zeros((tokens, wide - ff), BF16)
        for c in own:
            c.wait()
        part = sum(jnp.square(xg[row, :, i:i + 128].astype(F32)) for i in range(0, width, 128)).T
        sq[row] = jnp.sum(part, axis=0, keepdims=True)
    with jax.named_scope("barrier"):
        pl.semaphore_wait(barrier, 5)

    def cut(k):
        return pl.ds(pl.multiple_of(k * SLICE, SLICE), SLICE)

    def direct_slice(p):
        return y * (slices - RELAYED) + p if p < RELAYED else p

    def relayed_slice(q):
        return (1 - y) * (slices - RELAYED) + q

    def slice_of(item):
        return direct_slice(item[1]) if item[0] == "d" else relayed_slice(item[1])

    def parts(item):
        return (0, 1) if item[0] == "r" or item[1] < RELAYED else (None,)

    def x_block(b, item):
        toks = slice(None) if item[2] is None else pl.ds(item[2] * (tokens // 2), tokens // 2)
        return xg.at[b, toks, cut(slice_of(item))]

    x_in = {}
    pass_of = {item: i for i, (items, _) in enumerate(PASSES) for item in items}

    def send_x(p):
        for h in parts(("d", p)):
            x_in["d", p, h] = go(("xx", p, h), x_block(row, ("d", p, h)), far)

    for dev in (far, fsib, sib):
        go(("sq",), sq.at[row], dev)
    x_sib = go(("xs",), xg.at[row], sib)
    go(("gs",), gains.at[row], sib)
    send_x(0)
    for dev in (far, fsib):
        go(("g1",), gains.at[row, 0], dev)
    for p in range(1, DIRECT):
        send_x(p)
    for dev in (far, fsib):
        go(("g2",), gains.at[row, 1], dev)

    def norm_slice(b, k):
        cols = pl.ds(pl.multiple_of(b * width + k * SLICE, SLICE), SLICE)
        nb[:, cols] = (xg[b, :, cut(k)].astype(F32) * scale[...] * gains[b, 0, :, cut(k)]).astype(BF16)

    def norm_block(b):
        def step(k, carry):
            norm_slice(b, k)
            return carry
        lax.fori_loop(0, slices, step, 0)

    @scoped
    def relay(*item):
        x_in[item].wait_recv()
        blk = x_block(far_row, item)
        kind, p, h = item
        if kind == "d" and p < RELAYED:
            x_in["r", p, h] = go(("xy", p, h), blk, up)
        go(("xf", pass_of[kind, p]), blk, sib)

    with jax.named_scope("stats"):
        arrived(("sq",), sq.at[pl.ds(0, 3)])
        mean = (sq[0] + sq[1] + sq[2] + sq[3]) / hidden
        scale[...] = jnp.broadcast_to(lax.rsqrt(mean + NORM_EPS), (128, tokens)).T
    with jax.named_scope("norm_own"):
        norm_block(row)
    with jax.named_scope("norm_sib"):
        x_sib.wait_recv()
        arrived(("gs",), gains.at[0])
        norm_block(sib_row)

    near = pl.ds(pl.multiple_of(cx * 2 * width, 2 * width), 2 * width)
    for item in BESIDE[0]:
        relay(*item)
    for g, (c0, cn) in enumerate(NEAR):
        cols = slice(c0, c0 + cn)
        with jax.named_scope(f"gu_near#{g}"):
            loaded(("w", g), wg.at[pl.ds(0, 2 * cn)])
            gacc[cols] = dot_t(wg[cols, near], nb[:, near])
            uacc[cols] = dot_t(wu[cols, near], nb[:, near])
        for item in BESIDE[1 + g]:
            relay(*item)
    arrived(("g1",), gains.at[0])

    def send_a(t, c0, cn):
        go(("ax", t), ag.at[row, pl.ds(t * CHUNK, CHUNK), pl.ds(c0, cn)], far)

    for i, (items, relays) in enumerate(PASSES):
        with jax.named_scope(f"norm_pass#{i}"):
            for item in items:
                norm_slice(far_row, slice_of(item))
            arrived(("xf", i), xg.at[0, :, pl.ds(0, len(items) * SLICE)])
            for item in items:
                norm_slice(fsib_row, slice_of(item))
        where = [pl.ds(pl.multiple_of(b * width + slice_of(item) * SLICE, SLICE), SLICE)
                 for item in items for b in (far_row, fsib_row)]

        def product(w, cols):
            return dot_t(jnp.concatenate([w[cols, k] for k in where], axis=1), jnp.concatenate([nb[:, k] for k in where], axis=1))

        if i < len(PASSES) - 1:
            for g, (c0, cn) in enumerate(WIDE):
                cols = slice(c0, c0 + cn)
                with jax.named_scope(f"gu_pass#{i}#{g}"):
                    gate, upv = product(wg, cols), product(wu, cols)
                    gacc[cols] += gate
                    uacc[cols] += upv
                for item in relays[g]:
                    relay(*item)
            continue
        for g, (c0, cn) in enumerate(GROUPS):
            with jax.named_scope(f"gu_last#{g}"):
                cols = slice(c0, c0 + cn)
                gate = gacc[cols] + product(wg, cols)
                upv = uacc[cols] + product(wu, cols)
                ag[row, :, cols] = (jax.nn.silu(gate) * upv).astype(BF16).T
            sent_cn = cn if c0 + cn < ff else wide - c0
            for t in SPLIT_CHUNKS:
                send_a(t, c0, sent_cn)
            go(("as",), ag.at[row, :, pl.ds(c0, sent_cn)], sib)
    for t in range(CHUNKS):
        if t not in SPLIT_CHUNKS:
            send_a(t, 0, wide)

    @scoped
    def forward(t):
        blk = ag.at[far_row, pl.ds(t * CHUNK, CHUNK)]
        arrived(("ax", t), blk)
        go(("af", t), blk, sib)

    loaded(("wd",), wd)
    with jax.named_scope("down_own"):
        acc[...] = dot(ag[row, :, :ff], wd[row])
    with jax.named_scope("down_sib"):
        arrived(("as",), ag.at[sib_row])
        acc[...] += dot(ag[sib_row, :, :ff], wd[sib_row])

    rs, xp = {}, {}

    def halves(t):
        t0, tn = t * CHUNK, CHUNK
        hn = tn // 2
        return (pl.ds(pl.multiple_of(t0 + y * hn, hn), hn), pl.ds(pl.multiple_of(t0 + (1 - y) * hn, hn), hn),
                pl.ds(t0 // 2, hn))

    @scoped
    def down_far(t):
        rows = slice(t * CHUNK, (t + 1) * CHUNK)
        acc[rows] += dot(ag[far_row, rows, :ff], wd[far_row])

    @scoped
    def down_fsib(t):
        rows = slice(t * CHUNK, (t + 1) * CHUNK)
        arrived(("af", t), ag.at[fsib_row, pl.ds(t * CHUNK, CHUNK)])
        acc[rows] += dot(ag[fsib_row, rows, :ff], wd[fsib_row])
        _, other, packed = halves(t)
        rs[t] = go(("rs", t), acc.at[other], up, rbuf.at[packed])

    @scoped
    def combine(t):
        mine, _, packed = halves(t)
        rs[t].wait_recv()
        xn[row, mine] = (xg[row, mine].astype(F32) + (acc[mine] + rbuf[packed])).astype(BF16)
        blk = xn.at[row, mine]
        targets = [("y", up), ("x", far), ("s", sib)] + ([("d", diag)] if DIAGONAL[t] == "d" else [])
        for tag, dev in targets:
            xp[tag, t] = go(("xn", "s", t) if tag == "s" else ("xn", tag, t), blk, dev)

    @scoped
    def collect(tag, t):
        mine, other, _ = halves(t)
        r, rows = {"y": (row, other), "x": (far_row, mine), "d": (far_row, other)}[tag]
        xp[tag, t].wait_recv()
        blk = xn.at[r, rows]
        if (tag, DIAGONAL[t]) in (("y", "x"), ("x", "y")):
            xp["d", t] = go(("xn", "d", t), blk, far if tag == "y" else up)
        go(("xn", "s", t), blk, sib)

    @scoped
    def finish(t):
        t0, tn = t * CHUNK, CHUNK
        arrived(("xn", "s", t), xn.at[0, pl.ds(0, 2 * CHUNK)])
        res[pl.ds(t0, tn)] = xn[row, pl.ds(t0, tn)]

        def step(i, carry):
            rows = pl.ds(pl.multiple_of(t0 + i * 16, 16), 16)
            blocks = [xn[b, rows].astype(F32) for b in range(4)]
            total = sum(jnp.sum(v * v, axis=1, keepdims=True) for v in blocks)
            r = lax.rsqrt(total / hidden + NORM_EPS)
            for b in range(4):
                nb[rows, b * width:(b + 1) * width] = (blocks[b] * r * gains[b, 1]).astype(BF16)
            return carry
        lax.fori_loop(0, tn // 16, step, 0)

    @scoped
    def project(i):
        loaded(("wq",), wq)
        out[...] = dot(nb[:CUT * CHUNK], wq[...]).astype(BF16)

    arrived(("g2",), gains.at[0])
    steps = {"fwd": forward, "dfar": down_far, "dfs": down_fsib, "comb": combine, "cy": functools.partial(collect, "y"),
             "cx": functools.partial(collect, "x"), "cd": functools.partial(collect, "d"), "fin": finish, "proj": project}
    for name in STEPS:
        steps[name[:-1]](int(name[-1]))
    with jax.named_scope("drain"):
        pltpu.make_async_copy(sq.at[pl.ds(0, 3)], sq.at[pl.ds(0, 3)], send_sem.at[1]).wait()
        tiles = sum(sent) // (16 * 128 * 2)
        deep = max(d for d in range(1, ff // 16 + 1) if tiles % d == 0)
        like = wg.at[pl.ds(0, deep * 16), pl.ds(0, tiles // deep * 128)]
        pltpu.make_async_copy(like, like, send_sem.at[0]).wait()


def last_kernel(res, first, nb, wq, res_hbm, qkv_hbm, out, sem):
    t0, part = CUT * CHUNK, wq.shape[1] // 2
    copies = [pltpu.make_async_copy(res, res_hbm, sem.at[0]),
              pltpu.make_async_copy(first, qkv_hbm.at[pl.ds(0, t0)], sem.at[1])]
    for c in copies:
        c.start()
    for i in range(2):
        cols = pl.ds(i * part, part)
        out[:, cols] = dot(nb[t0:], wq[:, cols]).astype(BF16)
        c = pltpu.make_async_copy(out.at[:, cols], qkv_hbm.at[pl.ds(t0, out.shape[0]), cols], sem.at[2 + i])
        c.start()
        copies.append(c)
    for c in copies:
        c.wait()


def solution(mesh):
    def per_device(residual, gain_mlp, gain_attn, w_gate, w_up, w_down, w_qkv):
        tokens, width = residual.shape
        ff = w_gate.shape[1]
        qkv = w_qkv.shape[1]
        hidden = width * 4
        any_spec = pl.BlockSpec(memory_space=pl.ANY)
        vmem_spec = pl.BlockSpec(memory_space=pltpu.VMEM)
        held = pl.pallas_call(
            functools.partial(kernel, tokens, width, ff, Names(), Names()),
            out_shape=(pltpu.VMEM((tokens, width), BF16), pltpu.VMEM((CUT * CHUNK, qkv), BF16),
                       pltpu.VMEM((tokens, hidden), BF16), pltpu.VMEM((hidden, qkv), BF16)),
            in_specs=[any_spec] * 7,
            out_specs=(vmem_spec,) * 4,
            scratch_shapes=[
                pltpu.VMEM((4, tokens, width), BF16),
                pltpu.VMEM((ff, hidden), BF16),
                pltpu.VMEM((ff, hidden), BF16),
                pltpu.VMEM((4, ff, width), BF16),
                pltpu.VMEM((4, tokens, (ff + 127) // 128 * 128), BF16),
                pltpu.VMEM((tokens, width), F32),
                pltpu.VMEM((tokens // 2, width), F32),
                pltpu.VMEM((4, tokens, width), BF16),
                pltpu.VMEM((4, 2, 1, width), F32),
                pltpu.VMEM((4, 1, tokens), F32),
                pltpu.VMEM((tokens, 128), F32),
                pltpu.VMEM((ff, tokens), F32),
                pltpu.VMEM((ff, tokens), F32),
                pltpu.SemaphoreType.DMA((2,)),
                pltpu.SemaphoreType.DMA((81,)),
                pltpu.SemaphoreType.DMA((11,)),
            ],
            compiler_params=pltpu.CompilerParams(collective_id=0, has_side_effects=True, vmem_limit_bytes=50_000_000),
            name="block",
        )(residual, gain_mlp.reshape(1, width), gain_attn.reshape(1, width), w_gate.T, w_up.T, w_down, w_qkv)
        return pl.pallas_call(
            last_kernel,
            out_shape=(jax.ShapeDtypeStruct((tokens, width), BF16), jax.ShapeDtypeStruct((tokens, qkv), BF16)),
            in_specs=[vmem_spec] * 4,
            out_specs=(any_spec,) * 2,
            scratch_shapes=[pltpu.VMEM((tokens - CUT * CHUNK, qkv), BF16), pltpu.SemaphoreType.DMA((4,))],
            compiler_params=pltpu.CompilerParams(vmem_limit_bytes=16_000_000),
            name="last",
        )(*(pltpu.with_memory_space_constraint(v, pltpu.VMEM) for v in held))

    return jax.shard_map(
        per_device, mesh=mesh,
        in_specs=(P('data', 'row'), P('row'), P('row'), P(None, ('col', 'row')), P(None, ('col', 'row')),
                  P('col', 'row'), P(None, ('col', 'row'))),
        out_specs=(P('data', 'row'), P('data', ('col', 'row'))), check_vma=False)
```

time: 55.3 us -> 51.5 us (0.931)
  Pallas kernels: 52.9 us -> 50.6 us
  local copies, waits for them, and re-layouts: 1.67 us -> 0 us
    pallas_call x1, Pallas kernels: 52.9 us -> 48.1 us  [per_device(): pl.pallas_call(functools.partial(kernel, tokens, width, ff, Names(), Name...]
    pallas_call x0 -> x1, Pallas kernels: none -> 2.51 us  [per_device(): pl.pallas_call(last_kernel, out_shape=(jax.ShapeDtypeStruct((tokens, widt...]
    unnamed x2 -> x0, local copies, waits for them, and re-layouts: 1.67 us -> none
where the time goes in v3:
time: 51.5 us; the launch traced here: 51.4 us
  Pallas kernels  50.6 us (98%)
  between operations  0.8 us (2%)
    pallas_call x1, Pallas kernels, per_device(): pl.pallas_call(functools.partial(kernel, tokens, width, ff, Names(), Name...  48.1 us
    pallas_call x1, Pallas kernels, per_device(): pl.pallas_call(last_kernel, out_shape=(jax.ShapeDtypeStruct((tokens, widt...  2.51 us

profile of v3, /device:TPU:0, one launch (start us, length us, event | category | flops | bytes accessed | tf_op | source)
XLA Modules:
  0.0 51.4 jit_solution(8499781655271994872)
XLA Ops:
  0.6 48.1 %block.1 = (bf16[256,1024]{1,0:T(8,128)(2,1)S(1)}, bf16[128,1536]{1,0:T(8,128)(2,1)S(1)}, bf16[256,4096]{1,0:T(8,128)(2,1)S(1)}, bf16[4096,1536]{1,0:T(8,128)(2,1)S(1)}) custom-call(bf16[256,1024]{1,0:T(8,128)(2,1)} %x_hbm.1, f32[1,1024]{1,0:T(1,128)} %bitcast.6, f32[1,1024]{1,0:T(1,128)} %bitcast.7, bf16[1376,4096]{1,0:T(8,128)(2,1)} %bitcast.4, ...), custom_call_target="tpu_custom_call" | custom-call | tf_op jit(solution)/shard_map/block/pallas_call | solution.py:360
  48.7 2.5 %last.1 = (bf16[256,1024]{1,0:T(8,128)(2,1)}, bf16[256,1536]{1,0:T(8,128)(2,1)}) custom-call(bf16[256,1024]{1,0:T(8,128)(2,1)S(1)} %get-tuple-element.6.res, bf16[128,1536]{1,0:T(8,128)(2,1)S(1)} %get-tuple-element.7.first, bf16[256,4096]{1,0:T(8,128)(2,1)S(1)} %get-tuple-element.8.nb, bf16[4096,1536]{1,0:T(8,128)(2,1)S(1)} %get-tuple-element.9.wq), custom_call_target="tpu_custom_call" | custom-call | tf_op jit(solution)/shard_map/last/pallas_call | solution.py:387

commit v4 on v3

--- a/solution.py
+++ b/solution.py
@@ -24,15 +24,17 @@
           ((("d", 4), ("r", 2)), ()))
 CHUNK, CHUNKS = 32, 8
 SPLIT_CHUNKS = (0,)
-DIAGONAL = "xxxxxydd"
+DIAGONAL = "xxxxyxyd"
+LATE_PARTS = 1
 CUT = 4
 STEPS = (
-    "fwd0", "dfar0", "dfs0", "fwd1", "dfar1", "dfs1", "fwd2", "dfar2", "dfs2", "comb0", "fwd3", "dfar3",
-    "dfs3", "comb1", "fwd4", "dfar4", "dfs4", "comb2", "fwd5", "dfar5", "cy0", "dfs5", "comb3", "fwd6",
-    "dfar6", "cy1", "dfs6", "fwd7", "dfar7", "comb4", "cx0", "cy2", "dfs7", "cx1", "cx2", "comb5",
-    "cd0", "cy3", "cx3", "fin0", "cd1", "comb6", "cx4", "cy4", "fin1", "cd2", "cx5", "comb7",
-    "fin2", "cd3", "cy5", "cx6", "cy6", "fin3", "proj0", "cy7", "cd4", "cd5", "cd6", "cx7",
-    "fin4", "cd7", "fin5", "fin6", "fin7",
+    "fwd0", "dfar0", "dfs0", "fwd1", "dfar1", "dfs1", "fwd2", "dfar2", "dfs2", "comb0", "sy0", "fwd3",
+    "dfar3", "dfs3", "comb1", "sy1", "fwd4", "dfar4", "dfs4", "comb2", "sy2", "fwd5", "dfar5", "cy0",
+    "dfs5", "comb3", "sy3", "fwd6", "dfar6", "cy1", "dfs6", "fwd7", "comb4", "sy4", "dfar7", "cx0",
+    "cy2", "dfs7", "cx1", "cx2", "comb5", "sy5", "cd0", "cy3", "cx3", "fin0", "cd1", "comb6",
+    "sy6", "cx4", "cy4", "fin1", "cd2", "cx5", "comb7", "sy7", "fin2", "cd3", "cy5", "cx6",
+    "cy6", "fin3", "cd4", "proj0", "proj1", "cy7", "cx7", "fin4", "cd5", "cd6", "cd7", "proj2",
+    "fin5", "fin6", "fin7",
 )
 W_PARTS = 8
 
@@ -58,7 +60,20 @@
         self.table = {}
 
     def __call__(self, *key):
-        return self.table.setdefault(key, len(self.table))
+        return self.table.setdefault(earlier(key), len(self.table))
+
+
+def earlier(key):
+    if key[0] != "xn":
+        return key
+    tag, t = key[1:]
+    if tag == "x":
+        return ("xx",) + ((t // 2, t % 2) if t < 2 * RELAYED else (t - RELAYED, None))
+    if tag == "y":
+        return ("xy", t // 2, t % 2) if t < 2 * RELAYED else ("rs", t - 2 * RELAYED, 0)
+    if tag == "s":
+        return ("as",) if t == 0 else ("af", t - 1)
+    return ("xf", t) if t < len(PASSES) else (("sq",), ("xs",), ("gs",), ("g1",))[t - len(PASSES)]
 
 
 def kernel(tokens, width, ff, names, local_names,
@@ -258,8 +273,6 @@
         arrived(("as",), ag.at[sib_row])
         acc[...] += dot(ag[sib_row, :, :ff], wd[sib_row])
 
-    rs, xp = {}, {}
-
     def halves(t):
         t0, tn = t * CHUNK, CHUNK
         hn = tn // 2
@@ -271,32 +284,43 @@
         rows = slice(t * CHUNK, (t + 1) * CHUNK)
         acc[rows] += dot(ag[far_row, rows, :ff], wd[far_row])
 
+    def column_parts(t):
+        n = LATE_PARTS if t == CHUNKS - 1 else 1
+        return [pl.ds(i * (width // n), width // n) for i in range(n)]
+
     @scoped
     def down_fsib(t):
         rows = slice(t * CHUNK, (t + 1) * CHUNK)
         arrived(("af", t), ag.at[fsib_row, pl.ds(t * CHUNK, CHUNK)])
-        acc[rows] += dot(ag[fsib_row, rows, :ff], wd[fsib_row])
         _, other, packed = halves(t)
-        rs[t] = go(("rs", t), acc.at[other], up, rbuf.at[packed])
+        for i, cols in enumerate(column_parts(t)):
+            acc[rows, cols] += dot(ag[fsib_row, rows, :ff], wd[fsib_row, :, cols])
+            go(("rs", t, i), acc.at[other, cols], up, rbuf.at[packed, cols])
 
     @scoped
     def combine(t):
         mine, _, packed = halves(t)
-        rs[t].wait_recv()
-        xn[row, mine] = (xg[row, mine].astype(F32) + (acc[mine] + rbuf[packed])).astype(BF16)
-        blk = xn.at[row, mine]
-        targets = [("y", up), ("x", far), ("s", sib)] + ([("d", diag)] if DIAGONAL[t] == "d" else [])
-        for tag, dev in targets:
-            xp[tag, t] = go(("xn", "s", t) if tag == "s" else ("xn", tag, t), blk, dev)
+        for i, cols in enumerate(column_parts(t)):
+            arrived(("rs", t, i), rbuf.at[packed, cols])
+            xn[row, mine, cols] = (xg[row, mine, cols].astype(F32) + (acc[mine, cols] + rbuf[packed, cols])).astype(BF16)
+            blk = xn.at[row, mine, cols]
+            targets = ([("d", diag)] if DIAGONAL[t] == "d" else []) + [("x", far), ("s", sib)]
+            for tag, dev in targets:
+                go(("xn", tag, t), blk, dev)
+
+    @scoped
+    def send_up(t):
+        mine, _, _ = halves(t)
+        go(("xn", "y", t), xn.at[row, mine], up)
 
     @scoped
     def collect(tag, t):
         mine, other, _ = halves(t)
         r, rows = {"y": (row, other), "x": (far_row, mine), "d": (far_row, other)}[tag]
-        xp[tag, t].wait_recv()
         blk = xn.at[r, rows]
+        arrived(("xn", tag, t), blk)
         if (tag, DIAGONAL[t]) in (("y", "x"), ("x", "y")):
-            xp["d", t] = go(("xn", "d", t), blk, far if tag == "y" else up)
+            go(("xn", "d", t), blk, far if tag == "y" else up)
         go(("xn", "s", t), blk, sib)
 
     @scoped
@@ -313,15 +337,18 @@
             for b in range(4):
                 nb[rows, b * width:(b + 1) * width] = (blocks[b] * r * gains[b, 1]).astype(BF16)
             return carry
-        lax.fori_loop(0, tn // 16, step, 0)
+        lax.fori_loop(0, tn // 16, step, 0, unroll=True)
 
     @scoped
     def project(i):
-        loaded(("wq",), wq)
-        out[...] = dot(nb[:CUT * CHUNK], wq[...]).astype(BF16)
+        if i == 0:
+            loaded(("wq",), wq)
+        part = wq.shape[1] // 3
+        cols = slice(i * part, (i + 1) * part)
+        out[:, cols] = dot(nb[:CUT * CHUNK], wq[:, cols]).astype(BF16)
 
     arrived(("g2",), gains.at[0])
-    steps = {"fwd": forward, "dfar": down_far, "dfs": down_fsib, "comb": combine, "cy": functools.partial(collect, "y"),
+    steps = {"fwd": forward, "dfar": down_far, "dfs": down_fsib, "comb": combine, "sy": send_up, "cy": functools.partial(collect, "y"),
              "cx": functools.partial(collect, "x"), "cd": functools.partial(collect, "d"), "fin": finish, "proj": project}
     for name in STEPS:
         steps[name[:-1]](int(name[-1]))
@@ -378,8 +405,8 @@
                 pltpu.VMEM((ff, tokens), F32),
                 pltpu.VMEM((ff, tokens), F32),
                 pltpu.SemaphoreType.DMA((2,)),
-                pltpu.SemaphoreType.DMA((81,)),
-                pltpu.SemaphoreType.DMA((11,)),
+                pltpu.SemaphoreType.DMA((49,)),
+                pltpu.SemaphoreType.DMA((9,)),
             ],
             compiler_params=pltpu.CompilerParams(collective_id=0, has_side_effects=True, vmem_limit_bytes=50_000_000),
             name="block",

time: 51.5 us -> 50.3 us (0.977)
  Pallas kernels: 50.6 us -> 49.4 us
    pallas_call x1, Pallas kernels: 48.1 us -> 46.9 us  [per_device(): pl.pallas_call(functools.partial(kernel, tokens, width, ff, Names(), Name...]
where the time goes in v4:
time: 50.3 us; the launch traced here: 50.2 us
  Pallas kernels  49.4 us (98%)
  between operations  0.8 us (2%)
    pallas_call x1, Pallas kernels, per_device(): pl.pallas_call(functools.partial(kernel, tokens, width, ff, Names(), Name...  46.9 us
    pallas_call x1, Pallas kernels, per_device(): pl.pallas_call(last_kernel, out_shape=(jax.ShapeDtypeStruct((tokens, widt...  2.52 us

profile of v4, /device:TPU:0, one launch (start us, length us, event | category | flops | bytes accessed | tf_op | source)
XLA Modules:
  0.0 50.2 jit_solution(8492053226399015919)
XLA Ops:
  0.6 46.9 %block.1 = (bf16[256,1024]{1,0:T(8,128)(2,1)S(1)}, bf16[128,1536]{1,0:T(8,128)(2,1)S(1)}, bf16[256,4096]{1,0:T(8,128)(2,1)S(1)}, bf16[4096,1536]{1,0:T(8,128)(2,1)S(1)}) custom-call(bf16[256,1024]{1,0:T(8,128)(2,1)} %x_hbm.1, f32[1,1024]{1,0:T(1,128)} %bitcast.6, f32[1,1024]{1,0:T(1,128)} %bitcast.7, bf16[1376,4096]{1,0:T(8,128)(2,1)} %bitcast.4, ...), custom_call_target="tpu_custom_call" | custom-call | tf_op jit(solution)/shard_map/block/pallas_call | solution.py:387
  47.6 2.5 %last.1 = (bf16[256,1024]{1,0:T(8,128)(2,1)}, bf16[256,1536]{1,0:T(8,128)(2,1)}) custom-call(bf16[256,1024]{1,0:T(8,128)(2,1)S(1)} %get-tuple-element.6.res, bf16[128,1536]{1,0:T(8,128)(2,1)S(1)} %get-tuple-element.7.first, bf16[256,4096]{1,0:T(8,128)(2,1)S(1)} %get-tuple-element.8.nb, bf16[4096,1536]{1,0:T(8,128)(2,1)S(1)} %get-tuple-element.9.wq), custom_call_target="tpu_custom_call" | custom-call | tf_op jit(solution)/shard_map/last/pallas_call | solution.py:414

commit v5 on v4

--- a/solution.py
+++ b/solution.py
@@ -19,8 +19,8 @@
 GROUPS = ((0, 384), (384, 384), (768, 384), (1152, 224))
 BESIDE = ((("d", 0, 0),), (("d", 0, 1),), (("d", 1, 0),), (("d", 1, 1), ("d", 2, 0)), (("d", 2, 1), ("r", 0, 0)))
 PASSES = (((("d", 0), ("d", 1)), ((("r", 0, 1),), (("r", 1, 0), ("d", 3, None)))),
-          ((("d", 2), ("r", 0)), ((("r", 1, 1),), (("d", 4, None), ("r", 2, 0)))),
-          ((("d", 3), ("r", 1)), ((("r", 2, 1),), ())),
+          ((("d", 2), ("r", 0)), ((("r", 1, 1),), (("d", 4, None), ("r", 2, 0), ("r", 2, 1)))),
+          ((("d", 3), ("r", 1)), ((), ())),
           ((("d", 4), ("r", 2)), ()))
 CHUNK, CHUNKS = 32, 8
 SPLIT_CHUNKS = (0,)

time: 50.3 us -> 50 us (level)
  no operation moved by 1% of the time
where the time goes in v5:
time: 50 us; the launch traced here: 49.9 us
  Pallas kernels  49.1 us (98%)
  between operations  0.8 us (2%)
    pallas_call x1, Pallas kernels, per_device(): pl.pallas_call(functools.partial(kernel, tokens, width, ff, Names(), Name...  46.6 us
    pallas_call x1, Pallas kernels, per_device(): pl.pallas_call(last_kernel, out_shape=(jax.ShapeDtypeStruct((tokens, widt...  2.51 us

profile of v5, /device:TPU:0, one launch (start us, length us, event | category | flops | bytes accessed | tf_op | source)
XLA Modules:
  0.0 49.9 jit_solution(4718121121255026772)
XLA Ops:
  0.6 46.6 %block.1 = (bf16[256,1024]{1,0:T(8,128)(2,1)S(1)}, bf16[128,1536]{1,0:T(8,128)(2,1)S(1)}, bf16[256,4096]{1,0:T(8,128)(2,1)S(1)}, bf16[4096,1536]{1,0:T(8,128)(2,1)S(1)}) custom-call(bf16[256,1024]{1,0:T(8,128)(2,1)} %x_hbm.1, f32[1,1024]{1,0:T(1,128)} %bitcast.6, f32[1,1024]{1,0:T(1,128)} %bitcast.7, bf16[1376,4096]{1,0:T(8,128)(2,1)} %bitcast.4, ...), custom_call_target="tpu_custom_call" | custom-call | tf_op jit(solution)/shard_map/block/pallas_call | solution.py:387
  47.2 2.5 %last.1 = (bf16[256,1024]{1,0:T(8,128)(2,1)}, bf16[256,1536]{1,0:T(8,128)(2,1)}) custom-call(bf16[256,1024]{1,0:T(8,128)(2,1)S(1)} %get-tuple-element.6.res, bf16[128,1536]{1,0:T(8,128)(2,1)S(1)} %get-tuple-element.7.first, bf16[256,4096]{1,0:T(8,128)(2,1)S(1)} %get-tuple-element.8.nb, bf16[4096,1536]{1,0:T(8,128)(2,1)S(1)} %get-tuple-element.9.wq), custom_call_target="tpu_custom_call" | custom-call | tf_op jit(solution)/shard_map/last/pallas_call | solution.py:414

commit v6 on v5

--- a/solution.py
+++ b/solution.py
@@ -116,9 +116,13 @@
     own = [local(("x",), x_hbm, xg.at[row]), local(("g1",), g1_hbm, gains.at[row, 0]), local(("g2",), g2_hbm, gains.at[row, 1])]
     for c in own:
         c.start()
-    for g, (c0, cn) in enumerate(NEAR):
-        for src, dst in ((wg_hbm, wg), (wu_hbm, wu)):
-            local(("w", g), src.at[pl.ds(c0, cn)], dst.at[pl.ds(c0, cn)]).start()
+    near = pl.ds(pl.multiple_of(cx * 2 * width, 2 * width), 2 * width)
+    away = pl.ds(pl.multiple_of((1 - cx) * 2 * width, 2 * width), 2 * width)
+    for part in (near, away):
+        for g, (c0, cn) in enumerate(NEAR):
+            for src, dst in ((wg_hbm, wg), (wu_hbm, wu)):
+                key = ("w", g) if part is near else ("w", len(NEAR))
+                local(key, src.at[pl.ds(c0, cn), part], dst.at[pl.ds(c0, cn), part]).start()
     for i in range(4):
         local(("wd",), wd_hbm.at[pl.ds(i * ff, ff)], wd.at[i]).start()
     part = hidden // W_PARTS
@@ -207,18 +211,18 @@
         arrived(("gs",), gains.at[0])
         norm_block(sib_row)
 
-    near = pl.ds(pl.multiple_of(cx * 2 * width, 2 * width), 2 * width)
     for item in BESIDE[0]:
         relay(*item)
     for g, (c0, cn) in enumerate(NEAR):
         cols = slice(c0, c0 + cn)
         with jax.named_scope(f"gu_near#{g}"):
-            loaded(("w", g), wg.at[pl.ds(0, 2 * cn)])
+            loaded(("w", g), wg.at[pl.ds(0, cn)])
             gacc[cols] = dot_t(wg[cols, near], nb[:, near])
             uacc[cols] = dot_t(wu[cols, near], nb[:, near])
         for item in BESIDE[1 + g]:
             relay(*item)
     arrived(("g1",), gains.at[0])
+    loaded(("w", len(NEAR)), wg)
 
     def send_a(t, c0, cn):
         go(("ax", t), ag.at[row, pl.ds(t * CHUNK, CHUNK), pl.ds(c0, cn)], far)
@@ -237,7 +241,7 @@
             return dot_t(jnp.concatenate([w[cols, k] for k in where], axis=1), jnp.concatenate([nb[:, k] for k in where], axis=1))
 
         if i < len(PASSES) - 1:
-            for g, (c0, cn) in enumerate(WIDE):
+            for g, (c0, cn) in enumerate(WIDE if any(relays) else ((0, ff),)):
                 cols = slice(c0, c0 + cn)
                 with jax.named_scope(f"gu_pass#{i}#{g}"):
                     gate, upv = product(wg, cols), product(wu, cols)
@@ -406,7 +410,7 @@
                 pltpu.VMEM((ff, tokens), F32),
                 pltpu.SemaphoreType.DMA((2,)),
                 pltpu.SemaphoreType.DMA((49,)),
-                pltpu.SemaphoreType.DMA((9,)),
+                pltpu.SemaphoreType.DMA((10,)),
             ],
             compiler_params=pltpu.CompilerParams(collective_id=0, has_side_effects=True, vmem_limit_bytes=50_000_000),
             name="block",

time: 50 us -> 49.9 us (level)
  no operation moved by 1% of the time
where the time goes in v6:
time: 49.9 us; the launch traced here: 49.8 us
  Pallas kernels  49 us (98%)
  between operations  0.8 us (2%)
    pallas_call x1, Pallas kernels, per_device(): pl.pallas_call(functools.partial(kernel, tokens, width, ff, Names(), Name...  46.5 us
    pallas_call x1, Pallas kernels, per_device(): pl.pallas_call(last_kernel, out_shape=(jax.ShapeDtypeStruct((tokens, widt...  2.51 us

profile of v6, /device:TPU:0, one launch (start us, length us, event | category | flops | bytes accessed | tf_op | source)
XLA Modules:
  0.0 49.8 jit_solution(10972006174941768485)
XLA Ops:
  0.6 46.5 %block.1 = (bf16[256,1024]{1,0:T(8,128)(2,1)S(1)}, bf16[128,1536]{1,0:T(8,128)(2,1)S(1)}, bf16[256,4096]{1,0:T(8,128)(2,1)S(1)}, bf16[4096,1536]{1,0:T(8,128)(2,1)S(1)}) custom-call(bf16[256,1024]{1,0:T(8,128)(2,1)} %x_hbm.1, f32[1,1024]{1,0:T(1,128)} %bitcast.6, f32[1,1024]{1,0:T(1,128)} %bitcast.7, bf16[1376,4096]{1,0:T(8,128)(2,1)} %bitcast.4, ...), custom_call_target="tpu_custom_call" | custom-call | tf_op jit(solution)/shard_map/block/pallas_call | solution.py:391
  47.1 2.5 %last.1 = (bf16[256,1024]{1,0:T(8,128)(2,1)}, bf16[256,1536]{1,0:T(8,128)(2,1)}) custom-call(bf16[256,1024]{1,0:T(8,128)(2,1)S(1)} %get-tuple-element.6.res, bf16[128,1536]{1,0:T(8,128)(2,1)S(1)} %get-tuple-element.7.first, bf16[256,4096]{1,0:T(8,128)(2,1)S(1)} %get-tuple-element.8.nb, bf16[4096,1536]{1,0:T(8,128)(2,1)S(1)} %get-tuple-element.9.wq), custom_call_target="tpu_custom_call" | custom-call | tf_op jit(solution)/shard_map/last/pallas_call | solution.py:418

commit v7 on v6

--- a/solution.py
+++ b/solution.py
@@ -34,7 +34,7 @@
     "cy2", "dfs7", "cx1", "cx2", "comb5", "sy5", "cd0", "cy3", "cx3", "fin0", "cd1", "comb6",
     "sy6", "cx4", "cy4", "fin1", "cd2", "cx5", "comb7", "sy7", "fin2", "cd3", "cy5", "cx6",
     "cy6", "fin3", "cd4", "proj0", "proj1", "cy7", "cx7", "fin4", "cd5", "cd6", "cd7", "proj2",
-    "fin5", "fin6", "fin7",
+    "fin5", "fins6",
 )
 W_PARTS = 8
 
@@ -328,9 +328,10 @@
         go(("xn", "s", t), blk, sib)
 
     @scoped
-    def finish(t):
-        t0, tn = t * CHUNK, CHUNK
-        arrived(("xn", "s", t), xn.at[0, pl.ds(0, 2 * CHUNK)])
+    def finish(t, n=1):
+        t0, tn = t * CHUNK, n * CHUNK
+        for u in range(t, t + n):
+            arrived(("xn", "s", u), xn.at[0, pl.ds(0, 2 * CHUNK)])
         res[pl.ds(t0, tn)] = xn[row, pl.ds(t0, tn)]
 
         def step(i, carry):
@@ -353,7 +354,7 @@
 
     arrived(("g2",), gains.at[0])
     steps = {"fwd": forward, "dfar": down_far, "dfs": down_fsib, "comb": combine, "sy": send_up, "cy": functools.partial(collect, "y"),
-             "cx": functools.partial(collect, "x"), "cd": functools.partial(collect, "d"), "fin": finish, "proj": project}
+             "cx": functools.partial(collect, "x"), "cd": functools.partial(collect, "d"), "fin": finish, "fins": lambda t: finish(t, 2), "proj": project}
     for name in STEPS:
         steps[name[:-1]](int(name[-1]))
     with jax.named_scope("drain"):

time: 49.9 us -> 49.8 us (level)
  no operation moved by 1% of the time
where the time goes in v7:
time: 49.8 us; the launch traced here: 49.7 us
  Pallas kernels  48.9 us (98%)
  between operations  0.8 us (2%)
    pallas_call x1, Pallas kernels, per_device(): pl.pallas_call(functools.partial(kernel, tokens, width, ff, Names(), Name...  46.4 us
    pallas_call x1, Pallas kernels, per_device(): pl.pallas_call(last_kernel, out_shape=(jax.ShapeDtypeStruct((tokens, widt...  2.51 us

profile of v7, /device:TPU:0, one launch (start us, length us, event | category | flops | bytes accessed | tf_op | source)
XLA Modules:
  0.0 49.7 jit_solution(5231420264456993744)
XLA Ops:
  0.6 46.4 %block.1 = (bf16[256,1024]{1,0:T(8,128)(2,1)S(1)}, bf16[128,1536]{1,0:T(8,128)(2,1)S(1)}, bf16[256,4096]{1,0:T(8,128)(2,1)S(1)}, bf16[4096,1536]{1,0:T(8,128)(2,1)S(1)}) custom-call(bf16[256,1024]{1,0:T(8,128)(2,1)} %x_hbm.1, f32[1,1024]{1,0:T(1,128)} %bitcast.6, f32[1,1024]{1,0:T(1,128)} %bitcast.7, bf16[1376,4096]{1,0:T(8,128)(2,1)} %bitcast.4, ...), custom_call_target="tpu_custom_call" | custom-call | tf_op jit(solution)/shard_map/block/pallas_call | solution.py:392
  47.1 2.5 %last.1 = (bf16[256,1024]{1,0:T(8,128)(2,1)}, bf16[256,1536]{1,0:T(8,128)(2,1)}) custom-call(bf16[256,1024]{1,0:T(8,128)(2,1)S(1)} %get-tuple-element.6.res, bf16[128,1536]{1,0:T(8,128)(2,1)S(1)} %get-tuple-element.7.first, bf16[256,4096]{1,0:T(8,128)(2,1)S(1)} %get-tuple-element.8.nb, bf16[4096,1536]{1,0:T(8,128)(2,1)S(1)} %get-tuple-element.9.wq), custom_call_target="tpu_custom_call" | custom-call | tf_op jit(solution)/shard_map/last/pallas_call | solution.py:419
